TPU v7x, 256 devices: a whole 4x4x8 slice. The times are simulated.
256 devices in a mesh: data: 256 (over z, y, x, core).
Axes of the slice: x: 4, y: 4, z: 8, core: 2. Of those that a mesh axis runs over, the one named last changes fastest.
Arguments:
- act_in: bfloat16 [8192, 896], P('data')
- grad_top: bfloat16 [8192, 896], P('data')
- w_up: bfloat16 [2, 896, 4864], P(None, None, 'data')
- w_down: bfloat16 [2, 4864, 896], P(None, 'data')
- proj_up: bfloat16 [2, 896, 128], replicated
- proj_down: bfloat16 [2, 896, 128], replicated
- mom_up: float32 [2, 128, 4864], P(None, None, 'data')
- var_up: float32 [2, 128, 4864], P(None, None, 'data')
- mom_down: float32 [2, 4864, 128], P(None, 'data')
- var_down: float32 [2, 4864, 128], P(None, 'data')
Outputs:
- output 1: bfloat16 [2, 896, 4864], P(None, None, 'data')
- output 2: bfloat16 [2, 4864, 896], P(None, 'data')
- output 3: float32 [2, 128, 4864], P(None, None, 'data')
- output 4: float32 [2, 128, 4864], P(None, None, 'data')
- output 5: float32 [2, 4864, 128], P(None, 'data')
- output 6: float32 [2, 4864, 128], P(None, 'data')
All inputs are finite; a program needn't handle non-finite values.
Results may differ from a plain program's by a relative error of at most 0.00400308.
Values are sent between devices in bfloat16 or wider.
A program may use at most 768 MiB of HBM per device.

v0:
```python
import jax
import jax.numpy as jnp
from jax import lax
from jax.sharding import PartitionSpec as P

BETA_ONE = 0.9
BETA_TWO = 0.999
ADAM_EPS = 1e-8
STEP = 3
STEP_SCALE = 0.05


def contract_rows(left, right):
    return lax.dot_general(left, right, (((0,), (0,)), ((), ())), preferred_element_type=jnp.float32)


def contract_cols(left, right):
    return lax.dot_general(left, right, (((1,), (1,)), ((), ())), preferred_element_type=jnp.float32)


def adam_direction(grad_proj, moment, second):
    mom_new = BETA_ONE * moment + (1.0 - BETA_ONE) * grad_proj
    second_new = BETA_TWO * second + (1.0 - BETA_TWO) * grad_proj * grad_proj
    mom_hat = mom_new / (1.0 - BETA_ONE ** STEP)
    second_hat = second_new / (1.0 - BETA_TWO ** STEP)
    return mom_hat / (jnp.sqrt(second_hat) + ADAM_EPS), mom_new, second_new


def solution(mesh):
    def device_step(act_in, grad_top, w_up, w_down, proj_up, proj_down, mom_up, var_up, mom_down, var_down):
        layers = w_up.shape[0]
        step_size = STEP_SCALE / proj_up.shape[2] ** 0.5
        hidden = [act_in]
        pre_acts = []
        post_acts = []
        for layer_idx in range(layers):
            up_full = lax.all_gather(w_up[layer_idx], "data", axis=1, tiled=True)
            down_full = lax.all_gather(w_down[layer_idx], "data", axis=0, tiled=True)
            pre_act = jnp.dot(hidden[-1], up_full, preferred_element_type=jnp.float32)
            post_act = jax.nn.gelu(pre_act).astype(jnp.bfloat16)
            mlp_out = jnp.dot(post_act, down_full, preferred_element_type=jnp.float32)
            hidden.append((hidden[-1].astype(jnp.float32) + mlp_out).astype(jnp.bfloat16))
            pre_acts.append(pre_act)
            post_acts.append(post_act)
        grad_cur = grad_top
        new_up = [None] * layers
        new_down = [None] * layers
        mom_up_new = [None] * layers
        var_up_new = [None] * layers
        mom_down_new = [None] * layers
        var_down_new = [None] * layers
        for layer_idx in reversed(range(layers)):
            down_full = lax.all_gather(w_down[layer_idx], "data", axis=0, tiled=True)
            proj_up_f = proj_up[layer_idx].astype(jnp.float32)
            proj_down_f = proj_down[layer_idx].astype(jnp.float32)
            grad_down = contract_rows(post_acts[layer_idx], grad_cur)
            red_down_loc = jnp.dot(grad_down, proj_down_f, preferred_element_type=jnp.float32)
            red_down = lax.psum_scatter(red_down_loc, "data", scatter_dimension=0, tiled=True)
            d_post = contract_cols(grad_cur, down_full)
            _, gelu_back = jax.vjp(jax.nn.gelu, pre_acts[layer_idx])
            d_pre = gelu_back(d_post)[0].astype(jnp.bfloat16)
            grad_up = contract_rows(hidden[layer_idx], d_pre)
            red_up_loc = contract_rows(proj_up_f, grad_up)
            red_up = lax.psum_scatter(red_up_loc, "data", scatter_dimension=1, tiled=True)
            if layer_idx > 0:
                up_full = lax.all_gather(w_up[layer_idx], "data", axis=1, tiled=True)
                grad_cur = (grad_cur.astype(jnp.float32) + contract_cols(d_pre, up_full)).astype(jnp.bfloat16)
            dir_up, mom_a, var_a = adam_direction(red_up, mom_up[layer_idx], var_up[layer_idx])
            dir_down, mom_b, var_b = adam_direction(red_down, mom_down[layer_idx], var_down[layer_idx])
            up_step = jnp.dot(proj_up_f, dir_up, preferred_element_type=jnp.float32)
            down_step = contract_cols(dir_down, proj_down_f)
            new_up[layer_idx] = (w_up[layer_idx].astype(jnp.float32) - step_size * up_step).astype(jnp.bfloat16)
            new_down[layer_idx] = (w_down[layer_idx].astype(jnp.float32) - step_size * down_step).astype(jnp.bfloat16)
            mom_up_new[layer_idx] = mom_a
            var_up_new[layer_idx] = var_a
            mom_down_new[layer_idx] = mom_b
            var_down_new[layer_idx] = var_b
        return (jnp.stack(new_up), jnp.stack(new_down), jnp.stack(mom_up_new), jnp.stack(var_up_new), jnp.stack(mom_down_new), jnp.stack(var_down_new))

    tok_spec = P("data", None)
    col_spec = P(None, None, "data")
    row_spec = P(None, "data", None)
    return jax.shard_map(
        device_step,
        mesh=mesh,
        in_specs=(tok_spec, tok_spec, col_spec, row_spec, P(), P(), col_spec, col_spec, row_spec, row_spec),
        out_specs=(col_spec, row_spec, col_spec, col_spec, row_spec, row_spec),
        check_vma=False,
    )
```

profile of v0, /device:TPU:2, one launch (start us, length us, event | category | flops | bytes accessed | tf_op | source)
XLA Modules:
  0.0 867.1 jit_solution(8695920291729670057)
XLA Ops:
  7.2 1.7 fusion.198
  9.8 1.7 fusion.197
  12.1 129.0 %all-gather.11.cloned.1.call-done = bf16[1,896,4864]{1,0,2:T(2,128)(2,1)} async-done(((bf16[1,896,19]{1,0,2:T(2,128)(2,1)}), bf16[1,896,4864]{1,0,2:T(2,128)(2,1)}) %all-gather.11.cloned.1.call-update) | async-done | bytes 8716304 | tf_op jit(solution)/shard_map/all_gather | solution.py:37
  141.2 35.9 %copy.61 = bf16[1,896,4864]{2,1,0:T(8,128)(2,1)} copy(bf16[1,896,4864]{1,0,2:T(2,128)(2,1)} %all-gather.11.cloned.1.call-done) | data formatting | bytes 17432576 | tf_op jit(solution)/shard_map/all_gather | solution.py:37
  177.1 91.5 %all-gather.15.cloned.1.call-done = bf16[1,896,4864]{1,0,2:T(2,128)(2,1)} async-done(((bf16[1,896,19]{1,0,2:T(2,128)(2,1)}), bf16[1,896,4864]{1,0,2:T(2,128)(2,1)}) %all-gather.15.cloned.1.call-update) | async-done | bytes 8716304 | tf_op jit(solution)/shard_map/all_gather | solution.py:37
  268.6 35.8 %copy.66 = bf16[1,896,4864]{2,1,0:T(8,128)(2,1)} copy(bf16[1,896,4864]{1,0,2:T(2,128)(2,1)} %all-gather.15.cloned.1.call-done) | data formatting | bytes 17432576 | tf_op jit(solution)/shard_map/all_gather | solution.py:37
  304.4 4.7 fusion.11
  309.1 86.2 %all-gather.13.cloned.1.call-done = bf16[1,4864,896]{2,0,1:T(2,128)(2,1)} async-done(((bf16[1,19,896]{2,0,1:T(2,128)(2,1)}), bf16[1,4864,896]{2,0,1:T(2,128)(2,1)}) %all-gather.13.cloned.1.call-update) | async-done | bytes 8716304 | tf_op jit(solution)/shard_map/all_gather | solution.py:38
  395.3 7.5 fusion.34
  402.9 0.9 copy-done
  403.8 1.3 fusion.9
  405.1 116.9 %all-gather.9.cloned.1.call-done = bf16[1,4864,896]{2,0,1:T(2,128)(2,1)} async-done(((bf16[1,19,896]{2,0,1:T(2,128)(2,1)}), bf16[1,4864,896]{2,0,1:T(2,128)(2,1)}) %all-gather.9.cloned.1.call-update) | async-done | bytes 8716304 | tf_op jit(solution)/shard_map/all_gather | solution.py:53
  522.0 8.4 fusion.64
  530.4 6.1 fusion.31
  536.6 6.2 fusion.13
  542.8 6.4 fusion.16
  549.3 6.2 convolution_bitcast_fusion
  555.4 8.4 fusion.57
  564.0 6.5 convolution_bitcast_fusion.1
  570.6 280.6 %all-reduce.7.cloned.1.call-done = (f32[128,4864]{0,1:T(8,128)}, f32[128,4864]{0,1:T(8,128)}, f32[4864,128]{1,0:T(8,128)}, f32[4864,128]{1,0:T(8,128)}) async-done(((f32[128,4864]{0,1:T(8,128)}, f32[128,4864]{0,1:T(8,128)}, f32[4864,128]{1,0:T(8,128)}, f32[4864,128]{1,0:T(8,128)}), (f32[128,4864]{0,1:T(8,128)}, f32[128,4864]{0,1:T(8,128)}, f32[4864,128]{1,0:T(8,128)}, ...) | async-done | bytes 9961488
  851.2 0.9 fusion.49
  852.9 1.0 fusion.50
  853.9 1.0 fusion.47
  855.7 1.0 fusion.48
  (53 shorter events, 7.1 us)
Async XLA Ops:
  7.2 134.0 %all-gather.11.cloned.1.call-start = ((), (), s32[]{:S(2)}) async-start(), calls=%async_computation.1 | async-start | bytes 17500672 | tf_op jit(solution)/shard_map/all_gather | solution.py:37
  9.0 259.6 %all-gather.15.cloned.1.call-start = ((), (), s32[]{:S(2)}) async-start(), calls=%async_computation.3 | async-start | bytes 17500672 | tf_op jit(solution)/shard_map/all_gather | solution.py:37
  9.7 385.6 %all-gather.13.cloned.1.call-start = ((), (), s32[]{:S(2)}) async-start(), calls=%async_computation.2 | async-start | bytes 17500672 | tf_op jit(solution)/shard_map/all_gather | solution.py:38
  11.5 510.5 %all-gather.9.cloned.1.call-start = ((), (), s32[]{:S(2)}) async-start(), calls=%async_computation | async-start | bytes 17500672 | tf_op jit(solution)/shard_map/all_gather | solution.py:53
  12.1 839.1 %all-reduce.7.cloned.1.call-start = ((), (), s32[]{:S(2)}) async-start(), calls=%async_computation.4 | async-start | bytes 19922944
  177.1 127.3 %copy-start.5 = (bf16[32,896]{1,0:T(8,128)(2,1)S(1)}, bf16[32,896]{1,0:T(8,128)(2,1)}, u32[]{:S(2)}) copy-start(bf16[32,896]{1,0:T(8,128)(2,1)} %param.10) | copy-start | bytes 172036
  395.3 8.4 copy-start
  403.8 118.2 %copy-start.6 = (bf16[32,896]{1,0:T(8,128)(2,1)S(1)}, bf16[32,896]{1,0:T(8,128)(2,1)}, u32[]{:S(2)}) copy-start(bf16[32,896]{1,0:T(8,128)(2,1)} %param.11) | copy-start | bytes 172036
  405.1 131.5 %copy-start.11 = (bf16[2,896,128]{2,1,0:T(8,128)(2,1)S(1)}, bf16[2,896,128]{2,1,0:T(8,128)(2,1)}, u32[]{:S(2)}) copy-start(bf16[2,896,128]{2,1,0:T(8,128)(2,1)} %param.15) | copy-start | bytes 1376260
  536.6 12.7 %copy-start.12 = (bf16[2,896,128]{2,1,0:T(8,128)(2,1)S(1)}, bf16[2,896,128]{2,1,0:T(8,128)(2,1)}, u32[]{:S(2)}) copy-start(bf16[2,896,128]{2,1,0:T(8,128)(2,1)} %param.14) | copy-start | bytes 1376260
  563.9 6.6 copy-start.7
  563.9 6.6 copy-start.8
  563.9 6.6 copy-start.9
  563.9 6.6 copy-start.10
  563.9 287.2 %copy-start.4 = (bf16[1,19,896]{2,0,1:T(2,128)(2,1)S(1)}, bf16[1,19,896]{2,0,1:T(2,128)(2,1)}, u32[]{:S(2)}) copy-start(bf16[1,19,896]{2,0,1:T(2,128)(2,1)} %get-tuple-element.37) | copy-start | bytes 102148
  564.0 289.0 %copy-start.3 = (bf16[1,19,896]{2,0,1:T(2,128)(2,1)S(1)}, bf16[1,19,896]{2,0,1:T(2,128)(2,1)}, u32[]{:S(2)}) copy-start(bf16[1,19,896]{2,0,1:T(2,128)(2,1)} %get-tuple-element.36) | copy-start | bytes 102148
  564.0 289.9 %copy-start.2 = (bf16[1,896,19]{1,0,2:T(2,128)(2,1)S(1)}, bf16[1,896,19]{1,0,2:T(2,128)(2,1)}, u32[]{:S(2)}) copy-start(bf16[1,896,19]{1,0,2:T(2,128)(2,1)} %get-tuple-element.38) | copy-start | bytes 102148
  564.0 291.7 %copy-start.1 = (bf16[1,896,19]{1,0,2:T(2,128)(2,1)S(1)}, bf16[1,896,19]{1,0,2:T(2,128)(2,1)}, u32[]{:S(2)}) copy-start(bf16[1,896,19]{1,0,2:T(2,128)(2,1)} %get-tuple-element.39) | copy-start | bytes 102148
Sparse Core Ops, SparseCore 0:
  12.3 128.8 all-gather.10
  145.5 122.9 all-gather.14
  272.3 122.9 all-gather.12
  399.0 122.9 all-gather.8
  570.6 280.5 all-reduce.6
where the time goes:
time: 870 us; the launch traced here: 867 us
  waiting for transfers between devices  705 us (81%)
  local copies, waits for them, and re-layouts  80.1 us (9%)
  matrix products  65.7 us (8%)
  between operations  14 us (2%)
    unnamed x6, waiting for transfers between devices  282 us
    all_gather x2, waiting for transfers between devices, device_step(): up_full = lax.all_gather(w_up[layer_idx], 'data', axis=1, tiled=True)  221 us
    all_gather x2, waiting for transfers between devices, device_step(): down_full = lax.all_gather(w_down[layer_idx], 'data', axis=0, tiled=True)  203 us
    all_gather x2, local copies, waits for them, and re-layouts, device_step(): up_full = lax.all_gather(w_up[layer_idx], 'data', axis=1, tiled=True)  71.7 us
    dot_general x5, matrix products, contract_cols(): lax.dot_general(left, right, (((1,), (1,)), ((), ())), preferred_element_...  24.9 us
  transfers between devices with their start and end apart: 5, of which 5 were waited for; matrix products, arithmetic and copies ran while one was open for 10% of the time, Pallas kernels for 0%

commit v1 on v0

v1 whole, which is shorter than its diff:
```python
import jax
import jax.numpy as jnp
from jax import lax
from jax.experimental import pallas as pl
from jax.experimental.pallas import tpu as pltpu
from jax.sharding import PartitionSpec as P

BETA_ONE = 0.9
BETA_TWO = 0.999
ADAM_EPS = 1e-8
STEP = 3
STEP_SCALE = 0.05

NZ, NY, NX, NC = 8, 4, 4, 2
SLOTS = NY * NZ
SHARE = 19
ROWS = 40
KA = 512
BF16 = jnp.bfloat16
F32 = jnp.float32
GELU_C = 0.7978845608028654
GELU_A = 0.044715


def slot(dy, dz):
    return (dy % NY) * NZ + dz % NZ


def z_forward(part, dy, dz):
    dz %= NZ
    far_from_right = {0: part == 0, 1: True, 2: False, 3: False}[dy % NY]
    if dz == 0:
        return [("zm", 1), ("zp", NZ - 1)]
    if dz < 4:
        if dz < 3 or far_from_right:
            return [("zm", dz + 1)]
    elif dz > 4:
        if dz > 5 or not far_from_right:
            return [("zp", dz - 1)]
    return []


def y_forward(part, dy, dz):
    dy %= NY
    far_from_right = dz % 2 == 0
    if dy == 0:
        return [("ym", 1), ("yp", NY - 1)]
    if dy == 1 and far_from_right:
        return [("ym", 2)]
    if dy == 3 and not far_from_right:
        return [("yp", 2)]
    return []


def forwards(part, dy, dz):
    out = []
    if part == 0:
        if dy == 0:
            out += [(d, dy, n) for d, n in z_forward(part, dy, dz)]
        out += [(d, n, dz) for d, n in y_forward(part, dy, dz)]
    else:
        if dz == 0:
            out += [(d, n, dz) for d, n in y_forward(part, dy, dz)]
        out += [(d, dy, n) for d, n in z_forward(part, dy, dz)]
    return out


def wave_of(dy, dz):
    return min(dy, NY - dy) + min(dz, NZ - dz)


def check_tree():
    for part in (0, 1):
        got = set()
        for dy in range(NY):
            for dz in range(NZ):
                for _, ny, nz in forwards(part, dy, dz):
                    assert (ny % NY, nz % NZ) not in got
                    assert wave_of(ny % NY, nz % NZ) == wave_of(dy, dz) + 1
                    got.add((ny % NY, nz % NZ))
        assert len(got) == SLOTS - 1 and (0, 0) not in got


check_tree()


def nt(a, b):
    return lax.dot_general(a, b, (((1,), (1,)), ((), ())), preferred_element_type=F32)


def tn(a, b):
    return lax.dot_general(a, b, (((0,), (0,)), ((), ())), preferred_element_type=F32)


def nn(a, b):
    return lax.dot_general(a, b, (((1,), (0,)), ((), ())), preferred_element_type=F32)


def split(a):
    hi = a.astype(BF16)
    lo = (a - hi.astype(F32)).astype(BF16)
    return hi, lo


def kernel(h_ref, g_ref, xown_ref, pu_ref, pd_ref, m_ref, v_ref,
           w_out, m_out, v_out,
           xa, xb, h0, g1, h1, g0, xo, pq, mv, vv,
           act0, act1, gp0, dz0, dz1,
           part, rd, lbuf, rbuf, mid,
           rr, rmid, rl, rrt, zq, zbuf, res,
           wst, mst, vst,
           loc_sem, w_send, w_recv, ag_send, ag_recv, rs_send, rs_recv, r_send, r_recv, z_send, z_recv, out_sem):
    model = h_ref.shape[1]
    rank = pu_ref.shape[2]
    tok = h_ref.shape[0]
    group = NC * NX * tok
    step_size = STEP_SCALE / rank ** 0.5
    me = lax.axis_index("data")
    core = lax.rem(me, NC)
    x = lax.rem(lax.div(me, NC), NX)
    y = lax.rem(lax.div(me, NC * NX), NY)
    z = lax.div(me, NC * NX * NY)

    def dev(zz, yy, xx, cc):
        return ((lax.rem(zz, NZ) * NY + lax.rem(yy, NY)) * NX + lax.rem(xx, NX)) * NC + cc

    partner = dev(z, y, x, 1 - core)
    nbr = {
        "xp": dev(z, y, x + 1, core), "xm": dev(z, y, x + NX - 1, core),
        "yp": dev(z, y + 1, x, core), "ym": dev(z, y + NY - 1, x, core),
        "zp": dev(z + 1, y, x, core), "zm": dev(z + NZ - 1, y, x, core),
    }
    zdev = [None] + [dev(z + k, y, x, core) for k in range(1, NZ)]

    def remote(src, dst, ssem, rsem, target):
        return pltpu.make_async_remote_copy(
            src_ref=src, dst_ref=dst, send_sem=ssem, recv_sem=rsem,
            device_id=(target,), device_id_type=pl.DeviceIdType.MESH)

    local = []

    def stage(src, dst):
        copy = pltpu.make_async_copy(src, dst, loc_sem.at[len(local)])
        copy.start()
        local.append(copy)

    for layer in (0, 1):
        stage(xown_ref.at[layer, :, pl.ds(0, KA)], xa.at[layer, 0])
        stage(xown_ref.at[layer, :, pl.ds(KA, model - KA)], xb.at[layer, 0])
    stage(h_ref, h0.at[0, 0])
    stage(g_ref, g1.at[0, 0])
    stage(xown_ref, xo)
    for layer in (0, 1):
        stage(pu_ref.at[layer], pq.at[layer, :, pl.ds(0, rank)])
        stage(pd_ref.at[layer], pq.at[layer, :, pl.ds(rank, rank)])
    stage(m_ref, mv)
    stage(v_ref, vv)

    barrier = pltpu.get_barrier_semaphore()
    partners = [partner, nbr["xp"], nbr["xm"], nbr["yp"], nbr["ym"]] + zdev[1:]
    for target in partners:
        pl.semaphore_signal(barrier, inc=1, device_id=(target,), device_id_type=pl.DeviceIdType.MESH)
    pl.semaphore_wait(barrier, len(partners))
    for copy in local:
        copy.wait()

    wparts = (xa, xb)

    def w_issue(layer, prt, dy, dz):
        buf = wparts[prt]
        for direction, ny, nz in forwards(prt, dy, dz):
            remote(buf.at[layer, slot(dy, dz)], buf.at[layer, slot(ny, nz)],
                   w_send.at[layer, prt], w_recv.at[layer, prt, slot(ny, nz)], nbr[direction]).start()

    def w_own(layer):
        w_issue(layer, 0, 0, 0)
        w_issue(layer, 1, 0, 0)

    def w_wave(layer, wave):
        for dy in range(NY):
            for dz in range(NZ):
                if wave_of(dy, dz) == wave:
                    for prt in (0, 1):
                        s = slot(dy, dz)
                        buf = wparts[prt]
                        remote(buf.at[layer, s], buf.at[layer, s], w_send.at[layer, prt],
                               w_recv.at[layer, prt, s], partner).wait_recv()
                        w_issue(layer, prt, dy, dz)

    def w_drain(layer):
        for prt in (0, 1):
            buf = wparts[prt]
            remote(buf.at[layer, pl.ds(1, SLOTS - 1)], buf.at[layer, pl.ds(1, SLOTS - 1)],
                   w_send.at[layer, prt], w_recv.at[layer, prt, 0], partner).wait_send()

    half = tok // 2
    drains = []

    class Gather:
        def __init__(self, buf, index):
            self.buf, self.index = buf, index

        def copy(self, k, src, dst, target):
            return remote(src, dst, ag_send.at[self.index, k], ag_recv.at[self.index, k], target)

        def go(self, k, src, dst, target):
            copy = self.copy(k, src, dst, target)
            copy.start()
            drains.append(copy)

        def arrived(self, k, ref):
            self.copy(k, ref, ref, partner).wait_recv()

        def start(self):
            b = self.buf
            self.go(0, b.at[0, 0], b.at[0, 3], nbr["xp"])
            self.go(1, b.at[0, 0], b.at[0, 1], nbr["xm"])
            self.go(2, b.at[0, 0], b.at[1, 0], partner)

        def middle(self):
            b = self.buf
            lo, hi = pl.ds(0, half), pl.ds(half, half)
            self.arrived(0, b.at[0, 3])
            self.go(3, b.at[0, 3, lo], b.at[0, 2, lo], nbr["xp"])
            self.go(5, b.at[0, 3], b.at[1, 3], partner)
            self.arrived(1, b.at[0, 1])
            self.go(4, b.at[0, 1, hi], b.at[0, 2, hi], nbr["xm"])
            self.go(6, b.at[0, 1], b.at[1, 1], partner)

        def last(self):
            b = self.buf
            lo, hi = pl.ds(0, half), pl.ds(half, half)
            self.arrived(3, b.at[0, 2, lo])
            self.arrived(4, b.at[0, 2, hi])
            self.go(7, b.at[0, 2], b.at[1, 2], partner)

        def finish(self):
            b = self.buf
            self.arrived(2, b.at[1, 0])
            self.arrived(5, b.at[1, 3])
            self.arrived(6, b.at[1, 1])
            self.arrived(7, b.at[1, 2])

    class Reduce:
        def __init__(self, index):
            self.index = index

        def copy(self, k, src, dst, target):
            return remote(src, dst, rs_send.at[self.index, k], rs_recv.at[self.index, k], target)

        def go(self, k, src, dst, target):
            copy = self.copy(k, src, dst, target)
            copy.start()
            drains.append(copy)

        def arrived(self, k, ref):
            self.copy(k, ref, ref, partner).wait_recv()

        def to_partner(self):
            i = self.index
            self.go(0, part.at[i, 1], rd.at[i], partner)

        def ring(self):
            i = self.index
            lo, hi = pl.ds(0, half), pl.ds(half, half)
            self.arrived(0, rd.at[i])
            part[i, 0, 2] = part[i, 0, 2] + rd[i, 2]
            self.go(1, part.at[i, 0, 2, lo], mid.at[i, lo], nbr["xp"])
            self.go(2, part.at[i, 0, 2, hi], mid.at[i, hi], nbr["xm"])
            part[i, 0, 1] = part[i, 0, 1] + rd[i, 1]
            self.go(3, part.at[i, 0, 1, hi], lbuf.at[i, hi], nbr["xp"])
            part[i, 0, 3] = part[i, 0, 3] + rd[i, 3]
            self.go(4, part.at[i, 0, 3, lo], rbuf.at[i, lo], nbr["xm"])
            part[i, 0, 0] = part[i, 0, 0] + rd[i, 0]

        def ring_second(self):
            i = self.index
            lo, hi = pl.ds(0, half), pl.ds(half, half)
            self.arrived(1, mid.at[i, lo])
            part[i, 0, 1, lo] = part[i, 0, 1, lo] + mid[i, lo]
            self.go(5, part.at[i, 0, 1, lo], lbuf.at[i, lo], nbr["xp"])
            self.arrived(2, mid.at[i, hi])
            part[i, 0, 3, hi] = part[i, 0, 3, hi] + mid[i, hi]
            self.go(6, part.at[i, 0, 3, hi], rbuf.at[i, hi], nbr["xm"])

        def total(self):
            i = self.index
            lo, hi = pl.ds(0, half), pl.ds(half, half)
            self.arrived(3, lbuf.at[i, hi])
            self.arrived(4, rbuf.at[i, lo])
            self.arrived(5, lbuf.at[i, lo])
            self.arrived(6, rbuf.at[i, hi])
            return part[i, 0, 0] + lbuf[i] + rbuf[i]

    class Scatter:
        def __init__(self, layer):
            self.layer = layer

        def copy(self, k, src, dst, target):
            return remote(src, dst, r_send.at[self.layer, k], r_recv.at[self.layer, k], target)

        def go(self, k, src, dst, target):
            copy = self.copy(k, src, dst, target)
            copy.start()
            drains.append(copy)

        def arrived(self, k, ref):
            self.copy(k, ref, ref, partner).wait_recv()

        def ring(self):
            i = self.layer
            lo, hi = pl.ds(0, NZ // 2), pl.ds(NZ // 2, NZ // 2)
            self.go(0, rr.at[i, 2, lo], rmid.at[i, lo], nbr["yp"])
            self.go(1, rr.at[i, 2, hi], rmid.at[i, hi], nbr["ym"])
            self.go(2, rr.at[i, 1, hi], rl.at[i, hi], nbr["yp"])
            self.go(3, rr.at[i, 3, lo], rrt.at[i, lo], nbr["ym"])

        def ring_second(self):
            i = self.layer
            lo, hi = pl.ds(0, NZ // 2), pl.ds(NZ // 2, NZ // 2)
            self.arrived(0, rmid.at[i, lo])
            rr[i, 1, lo] = rr[i, 1, lo] + rmid[i, lo]
            self.go(4, rr.at[i, 1, lo], rl.at[i, lo], nbr["yp"])
            self.arrived(1, rmid.at[i, hi])
            rr[i, 3, hi] = rr[i, 3, hi] + rmid[i, hi]
            self.go(5, rr.at[i, 3, hi], rrt.at[i, hi], nbr["ym"])

        def along_z(self):
            i = self.layer
            lo, hi = pl.ds(0, NZ // 2), pl.ds(NZ // 2, NZ // 2)
            self.arrived(2, rl.at[i, hi])
            self.arrived(3, rrt.at[i, lo])
            self.arrived(4, rl.at[i, lo])
            self.arrived(5, rrt.at[i, hi])
            zq[i] = rr[i, 0] + rl[i] + rrt[i]
            for k in (4, 3, 5, 2, 6, 1, 7):
                copy = remote(zq.at[i, k], zbuf.at[i, NZ - k], z_send.at[i, k], z_recv.at[i, NZ - k], zdev[k])
                copy.start()
                drains.append(copy)

        def total(self):
            i = self.layer
            out = zq[i, 0]
            for k in range(1, NZ):
                remote(zbuf.at[i, k], zbuf.at[i, k], z_send.at[i, k], z_recv.at[i, k], partner).wait_recv()
                out = out + zbuf[i, k]
            return out

    rows = SLOTS * ROWS
    CH = 640
    per = CH // ROWS

    def xrows(layer, i):
        a = xa[layer, pl.ds(i * per, per)].reshape(CH, KA)
        b = xb[layer, pl.ds(i * per, per)].reshape(CH, model - KA)
        return a, b

    def against(x2, acts):
        return nt(x2[0], acts[:, :KA]) + nt(x2[1], acts[:, KA:])

    def row_in_slot():
        r = lax.broadcasted_iota(jnp.int32, (CH, group), 0)
        return lax.rem(r, ROWS)

    def chunks(body):
        def step(i, carry):
            body(i)
            return carry
        lax.fori_loop(0, rows // CH, step, 0)

    def gelu_pair(zt):
        sq = zt * zt
        t = jnp.tanh(GELU_C * (zt + GELU_A * (zt * sq)))
        half_one = 0.5 * (1.0 + t)
        value = zt * half_one
        slope = half_one + 0.5 * zt * (1.0 - t * t) * (GELU_C * (1.0 + 3.0 * GELU_A * sq))
        return value, slope

    def to_down(v):
        r = row_in_slot()
        keep = jnp.logical_and(r >= SHARE, r < 2 * SHARE)
        return jnp.where(keep, pltpu.roll(v, SHARE, 0), 0.0)

    def to_up(v):
        return pltpu.roll(v, CH - SHARE, 0)

    def mask_up(v):
        return jnp.where(row_in_slot() < SHARE, v, 0.0)

    def block(i):
        return pl.ds(pl.multiple_of(i * CH, CH), CH)

    def products(act_ref, layer, out_index):
        def body(j):
            for q in range(1, -1, -1):
                pass
        for cc in (1, 0):
            toks = pl.ds(cc * (group // 2), group // 2)
            lhs = act_ref[:, toks]
            a = xa[layer].reshape(rows, KA)
            b = xb[layer].reshape(rows, model - KA)
            part[out_index, cc, :, :, pl.ds(0, KA)] = tn(lhs, a).reshape(NX, tok, KA)
            part[out_index, cc, :, :, pl.ds(KA, model - KA)] = tn(lhs, b).reshape(NX, tok, model - KA)
            if cc == 1:
                Reduce(out_index).to_partner()

    def flat(ref):
        return ref[...].reshape(group, model)

    def project(layer, h_ref2, g_ref2):
        hp = nn(flat(h_ref2), pq[layer])[:, :rank]
        gq = nn(flat(g_ref2), pq[layer])[:, rank:]
        return jnp.concatenate(split(hp), axis=1), jnp.concatenate(split(gq), axis=1)

    gather_h, gather_g = Gather(h0, 0), Gather(g1, 1)
    w_own(0)
    gather_h.start()
    w_own(1)
    gather_g.start()
    w_wave(0, 1)
    gather_h.middle()
    w_wave(0, 2)
    w_wave(1, 1)
    gather_h.last()
    gather_g.middle()
    w_wave(0, 3)
    w_wave(1, 2)
    gather_g.last()
    gather_h.finish()
    w_wave(0, 4)
    w_wave(1, 3)
    gather_g.finish()
    w_wave(0, 5)
    w_wave(1, 4)
    w_wave(0, 6)

    acts = flat(h0)

    @chunks
    def _(i):
        zt = against(xrows(0, i), flat(h0))
        value, slope = gelu_pair(zt)
        gp0[block(i), :] = slope
        act0[block(i), :] = to_down(value).astype(BF16)

    products(act0, 0, 0)
    w_wave(1, 5)
    reduce0 = Reduce(0)
    reduce0.ring()
    reduce0.ring_second()
    w_wave(1, 6)
    h1[0, 0] = (h0[0, 0].astype(F32) + reduce0.total()).astype(BF16)
    gather1 = Gather(h1, 2)
    gather1.start()
    gather1.middle()
    gather1.last()
    gather1.finish()

    @chunks
    def _(i):
        x2 = xrows(1, i)
        value, slope = gelu_pair(against(x2, flat(h1)))
        act1[block(i), :] = to_down(value).astype(BF16)
        dpost = to_up(against(x2, flat(g1)))
        dz1[block(i), :] = mask_up(slope * dpost).astype(BF16)

    products(dz1, 1, 1)
    reduce1 = Reduce(1)

    def projected(layer, dz_ref, act_ref, h_ref2, g_ref2):
        hp, gq = project(layer, h_ref2, g_ref2)

        @chunks
        def _(i):
            both = nn(dz_ref[block(i), :], hp) + nn(act_ref[block(i), :], gq)
            both = both[:, :rank] + both[:, rank:]
            both = both.reshape(per // NZ, NZ, ROWS, rank)
            rr[layer, pl.ds(i * (per // NZ), per // NZ)] = both

    reduce1.ring()
    reduce1.ring_second()
    projected(1, dz1, act1, h1, g1)
    scatter1 = Scatter(1)
    scatter1.ring()
    g0[0, 0] = (g1[0, 0].astype(F32) + reduce1.total()).astype(BF16)
    gather0 = Gather(g0, 3)
    gather0.start()
    scatter1.ring_second()
    gather0.middle()
    gather0.last()
    gather0.finish()

    @chunks
    def _(i):
        dpost = to_up(against(xrows(0, i), flat(g0)))
        dz0[block(i), :] = mask_up(gp0[block(i), :] * dpost).astype(BF16)

    projected(0, dz0, act0, h0, g0)
    scatter0 = Scatter(0)
    scatter0.ring()
    scatter1.along_z()

    def update(layer, red):
        mom = BETA_ONE * mv[layer] + (1.0 - BETA_ONE) * red
        var = BETA_TWO * vv[layer] + (1.0 - BETA_TWO) * red * red
        direction = (mom / (1.0 - BETA_ONE ** STEP)) / (jnp.sqrt(var / (1.0 - BETA_TWO ** STEP)) + ADAM_EPS)
        mst[layer] = mom
        vst[layer] = var
        r = lax.broadcasted_iota(jnp.int32, (ROWS, rank), 0)
        up = jnp.where(r < SHARE, direction, 0.0)
        down = jnp.where(r >= SHARE, direction, 0.0)
        both = jnp.concatenate([up, down], axis=1)
        hi, lo = split(both)
        change = nt(jnp.concatenate([hi, lo], axis=0), pq[layer])
        change = change[:ROWS] + change[ROWS:]
        wst[layer] = (xo[layer].astype(F32) - step_size * change).astype(BF16)

    scatter0.ring_second()
    scatter0.along_z()
    update(1, scatter1.total())
    update(0, scatter0.total())

    outs = [(wst, w_out), (mst, m_out), (vst, v_out)]
    copies = [pltpu.make_async_copy(src, dst, out_sem.at[k]) for k, (src, dst) in enumerate(outs)]
    for copy in copies:
        copy.start()
    w_drain(0)
    w_drain(1)
    for copy in drains:
        copy.wait_send()
    for copy in copies:
        copy.wait()


def fused_step(act_in, grad_top, xown, proj_up, proj_down, mom, var):
    tok, model = act_in.shape
    layers, _, rank = proj_up.shape
    kb = model - KA
    group = NC * NX * tok
    rows = SLOTS * ROWS
    dma = pltpu.SemaphoreType.DMA
    anyspace = pl.BlockSpec(memory_space=pl.ANY)
    vm = pltpu.VMEM
    blk = (NC, NX, tok, model)
    scratch = [
        vm((2, SLOTS, ROWS, KA), BF16), vm((2, SLOTS, ROWS, kb), BF16),
        vm(blk, BF16), vm(blk, BF16), vm(blk, BF16), vm(blk, BF16),
        vm((2, ROWS, model), BF16), vm((2, model, 2 * rank), BF16), vm((2, ROWS, rank), F32), vm((2, ROWS, rank), F32),
        vm((rows, group), BF16), vm((rows, group), BF16), vm((rows, group), F32), vm((rows, group), BF16), vm((rows, group), BF16),
        vm((2,) + blk, F32), vm((2, NX, tok, model), F32), vm((2, tok, model), F32), vm((2, tok, model), F32), vm((2, tok, model), F32),
        vm((2, NY, NZ, ROWS, rank), F32), vm((2, NZ, ROWS, rank), F32), vm((2, NZ, ROWS, rank), F32), vm((2, NZ, ROWS, rank), F32),
        vm((2, NZ, ROWS, rank), F32), vm((2, NZ, ROWS, rank), F32), vm((2, ROWS, rank), F32),
        vm((2, ROWS, model), BF16), vm((2, ROWS, rank), F32), vm((2, ROWS, rank), F32),
        dma((13,)), dma((2, 2)), dma((2, 2, SLOTS)), dma((4, 8)), dma((4, 8)), dma((2, 7)), dma((2, 7)),
        dma((2, 6)), dma((2, 6)), dma((2, NZ)), dma((2, NZ)), dma((3,)),
    ]
    return pl.pallas_call(
        kernel,
        name="galore_step",
        out_shape=(jax.ShapeDtypeStruct((2, ROWS, model), BF16), jax.ShapeDtypeStruct((2, ROWS, rank), F32),
                   jax.ShapeDtypeStruct((2, ROWS, rank), F32)),
        in_specs=[anyspace] * 7,
        out_specs=(anyspace,) * 3,
        scratch_shapes=scratch,
        compiler_params=pltpu.CompilerParams(collective_id=0, has_side_effects=True, vmem_limit_bytes=48 * 1024 * 1024),
    )(act_in, grad_top, xown, proj_up, proj_down, mom, var)


def solution(mesh):
    def pack(up, down):
        up = up.transpose(0, 2, 1)
        pad = jnp.zeros((up.shape[0], ROWS - 2 * SHARE, up.shape[2]), up.dtype)
        return jnp.concatenate([up, down, pad], axis=1)

    def unpack(packed):
        return packed[:, :SHARE].transpose(0, 2, 1), packed[:, SHARE:2 * SHARE]

    def device_step(act_in, grad_top, w_up, w_down, proj_up, proj_down, mom_up, var_up, mom_down, var_down):
        w_new, m_new, v_new = fused_step(act_in, grad_top, pack(w_up, w_down), proj_up, proj_down,
                                         pack(mom_up, mom_down), pack(var_up, var_down))
        new_up, new_down = unpack(w_new)
        new_mom_up, new_mom_down = unpack(m_new)
        new_var_up, new_var_down = unpack(v_new)
        return new_up, new_down, new_mom_up, new_var_up, new_mom_down, new_var_down

    tok_spec = P("data", None)
    col_spec = P(None, None, "data")
    row_spec = P(None, "data", None)
    return jax.shard_map(
        device_step,
        mesh=mesh,
        in_specs=(tok_spec, tok_spec, col_spec, row_spec, P(), P(), col_spec, col_spec, row_spec, row_spec),
        out_specs=(col_spec, row_spec, col_spec, col_spec, row_spec, row_spec),
        check_vma=False,
    )
```

time: 870 us -> 105 us (0.12)
  waiting for transfers between devices: 705 us -> 0 us
  Pallas kernels: 0 us -> 95.3 us
  local copies, waits for them, and re-layouts: 80.1 us -> 8.21 us
  matrix products: 65.7 us -> 0 us
  between operations: 14 us -> 0.72 us
    all_gather x4 -> x0, waiting for transfers between devices: 424 us -> none  [the longest x2 221 us: device_step(): up_full = lax.all_gather(w_up[layer_idx], 'data', axis=1, tiled=True)]
    unnamed x6 -> x0, waiting for transfers between devices: 282 us -> none
    pallas_call x0 -> x1, Pallas kernels: none -> 95.3 us  [fused_step(): pl.pallas_call(kernel, name='galore_step', out_shape=(jax.ShapeDtypeStruc...]
    all_gather x2 -> x0, local copies, waits for them, and re-layouts: 71.7 us -> none  [device_step(): up_full = lax.all_gather(w_up[layer_idx], 'data', axis=1, tiled=True)]
    dot_general x14 -> x0, matrix products: 65.7 us -> none  [the longest x5 24.9 us: contract_cols(): lax.dot_general(left, right, (((1,), (1,)), ((), ())), preferred_element_...]
  transfers between devices with their start and end apart: 5 -> 0, of which waited for: 5 -> 0; matrix products, arithmetic and copies ran while one was open for 10% -> 0% of each run, Pallas kernels for 0% -> 0%
where the time goes in v1:
time: 105 us; the launch traced here: 104 us
  Pallas kernels  95.3 us (91%)
  local copies, waits for them, and re-layouts  8.21 us (8%)
    pallas_call x1, Pallas kernels, fused_step(): pl.pallas_call(kernel, name='galore_step', out_shape=(jax.ShapeDtypeStruc...  95.3 us
    unnamed x20, local copies, waits for them, and re-layouts  7.19 us

profile of v1, /device:TPU:2, one launch (start us, length us, event | category | flops | bytes accessed | tf_op | source)
XLA Modules:
  0.0 104.4 jit_solution(15256992573594611798)
XLA Ops:
  0.6 0.1 pad.8.clone
  0.7 0.0 copy-start.4
  0.7 0.1 pad.5.clone
  0.8 0.0 copy-start.2
  0.8 0.7 copy.19
  1.5 0.0 copy-done.4
  1.5 0.0 copy-start
  1.6 0.8 copy_bitcast_fusion.1
  2.4 0.1 maximum_maximum_fusion.2
  2.5 0.9 copy.31
  3.4 0.9 copy.17
  4.3 0.1 maximum_maximum_fusion.xown_ref
  4.4 0.0 copy-done.2
  4.4 0.0 copy-done.1
  4.4 0.0 copy-done
  4.4 0.0 copy-start.3
  4.4 0.8 copy-done.3
  5.2 95.3 %galore_step.1 = (bf16[2,40,896]{2,1,0:T(8,128)(2,1)S(1)}, f32[2,40,128]{2,1,0:T(8,128)S(1)}, f32[2,40,128]{2,1,0:T(8,128)S(1)}) custom-call(bf16[32,896]{1,0:T(8,128)(2,1)S(1)} %copy-done.2, bf16[32,896]{1,0:T(8,128)(2,1)S(1)} %copy-done.3, bf16[2,40,896]{2,1,0:T(8,128)(2,1)S(1)} %maximum_maximum_fusion.xown_ref, bf16[2,896,128]{2,1,0:T(8,128)(2,1)S(1)} %copy-done, ...), custom_call_target="tpu_custom_call" | custom-call | tf_op jit(solution)/shard_map/galore_step/pallas_call | solution.py:557
  100.6 0.7 copy.23
  101.3 0.6 copy.26
  101.9 0.6 copy.24
  102.5 0.6 copy.27
  103.1 0.6 copy.25
  103.7 0.7 copy.22
  (7 shorter events, 0.0 us)
Async XLA Ops:
  0.7 0.8 copy-start.4
  0.8 3.6 %copy-start.2 = (bf16[32,896]{1,0:T(8,128)(2,1)S(1)}, bf16[32,896]{1,0:T(8,128)(2,1)}, u32[]{:S(2)}) copy-start(bf16[32,896]{1,0:T(8,128)(2,1)} %h_ref.1) | copy-start | bytes 172036
  1.5 2.8 %copy-start.1 = (bf16[2,896,128]{2,1,0:T(8,128)(2,1)S(1)}, bf16[2,896,128]{2,1,0:T(8,128)(2,1)}, u32[]{:S(2)}) copy-start(bf16[2,896,128]{2,1,0:T(8,128)(2,1)} %pd_ref.1) | copy-start | bytes 1376260
  1.5 2.8 %copy-start = (bf16[2,896,128]{2,1,0:T(8,128)(2,1)S(1)}, bf16[2,896,128]{2,1,0:T(8,128)(2,1)}, u32[]{:S(2)}) copy-start(bf16[2,896,128]{2,1,0:T(8,128)(2,1)} %pu_ref.1) | copy-start | bytes 1376260
  4.4 0.8 copy-start.3

commit v2 on v1

--- a/solution.py
+++ b/solution.py
@@ -1,3 +1,5 @@
+import heapq
+
 import jax
 import jax.numpy as jnp
 from jax import lax
@@ -15,7 +17,7 @@
 SLOTS = NY * NZ
 SHARE = 19
 ROWS = 40
-KA = 512
+PARTS = ((0, 256, True, 0), (256, 256, True, 1), (512, 256, False, 0), (768, 128, False, 1))
 BF16 = jnp.bfloat16
 F32 = jnp.float32
 GELU_C = 0.7978845608028654
@@ -26,62 +28,78 @@
     return (dy % NY) * NZ + dz % NZ
 
 
-def z_forward(part, dy, dz):
+def forwards(prt, dy, dz):
+    _, _, z_first, variant = PARTS[prt]
+    dy %= NY
     dz %= NZ
-    far_from_right = {0: part == 0, 1: True, 2: False, 3: False}[dy % NY]
+    far_z = (variant == 0) if z_first else (dy < 2) == (variant == 0)
+    far_y = (dz + variant) % 2 == 0
+    along_z, along_y = [], []
     if dz == 0:
-        return [("zm", 1), ("zp", NZ - 1)]
-    if dz < 4:
-        if dz < 3 or far_from_right:
-            return [("zm", dz + 1)]
-    elif dz > 4:
-        if dz > 5 or not far_from_right:
-            return [("zp", dz - 1)]
-    return []
-
-
-def y_forward(part, dy, dz):
-    dy %= NY
-    far_from_right = dz % 2 == 0
+        along_z = [("zm", dy, 1), ("zp", dy, NZ - 1)]
+    elif dz < 4 and (dz < 3 or far_z):
+        along_z = [("zm", dy, dz + 1)]
+    elif dz > 4 and (dz > 5 or not far_z):
+        along_z = [("zp", dy, dz - 1)]
     if dy == 0:
-        return [("ym", 1), ("yp", NY - 1)]
-    if dy == 1 and far_from_right:
-        return [("ym", 2)]
-    if dy == 3 and not far_from_right:
-        return [("yp", 2)]
-    return []
-
-
-def forwards(part, dy, dz):
-    out = []
-    if part == 0:
-        if dy == 0:
-            out += [(d, dy, n) for d, n in z_forward(part, dy, dz)]
-        out += [(d, n, dz) for d, n in y_forward(part, dy, dz)]
-    else:
-        if dz == 0:
-            out += [(d, n, dz) for d, n in y_forward(part, dy, dz)]
-        out += [(d, dy, n) for d, n in z_forward(part, dy, dz)]
+        along_y = [("ym", 1, dz), ("yp", NY - 1, dz)]
+    elif (dy == 1 and far_y):
+        along_y = [("ym", 2, dz)]
+    elif (dy == 3 and not far_y):
+        along_y = [("yp", 2, dz)]
+    if z_first:
+        return (along_z if dy == 0 else []) + along_y
+    return (along_y if dz == 0 else []) + along_z
+
+
+def path_left(prt, dy, dz):
+    nxt = forwards(prt, dy, dz)
+    return 1 + max(path_left(prt, ny, nz) for _, ny, nz in nxt) if nxt else 0
+
+
+def weight_order(latency=1.75, rate=46600.0, late=6.0):
+    queues = {d: [] for d in ("zp", "zm", "yp", "ym")}
+    free = dict.fromkeys(queues, 0.0)
+    events, out, count = [], [], 0
+
+    def push(t, kind, data):
+        nonlocal count
+        heapq.heappush(events, (t, count, kind, data))
+        count += 1
+
+    def arrive(t, layer, prt, dy, dz):
+        nonlocal count
+        for d, ny, nz in forwards(prt, dy, dz):
+            queues[d].append((layer, -path_left(prt, ny, nz), count, prt, dy, dz, ny, nz))
+            count += 1
+            push(t, "kick", d)
+
+    push(0.0, "own", 0)
+    push(late, "own", 1)
+    while events:
+        t, _, kind, data = heapq.heappop(events)
+        if kind == "own":
+            for prt in range(len(PARTS)):
+                arrive(t, data, prt, 0, 0)
+        elif kind == "kick":
+            if free[data] <= t + 1e-9 and queues[data]:
+                queues[data].sort()
+                layer, _, _, prt, dy, dz, ny, nz = queues[data].pop(0)
+                out.append((t, "send", layer, prt, dy, dz, data, ny, nz))
+                free[data] = t + 2 * ROWS * PARTS[prt][1] / rate
+                push(free[data], "kick", data)
+                push(free[data] + latency, "arrive", (layer, prt, ny, nz))
+        else:
+            out.append((t, "wait", *data, None, None, None))
+            arrive(t, *data)
+    for layer in (0, 1):
+        for prt in range(len(PARTS)):
+            got = [e[4:6] for e in out if e[1:4] == ("wait", layer, prt)]
+            assert len(got) == len(set(got)) == SLOTS - 1 and (0, 0) not in got
     return out
 
 
-def wave_of(dy, dz):
-    return min(dy, NY - dy) + min(dz, NZ - dz)
-
-
-def check_tree():
-    for part in (0, 1):
-        got = set()
-        for dy in range(NY):
-            for dz in range(NZ):
-                for _, ny, nz in forwards(part, dy, dz):
-                    assert (ny % NY, nz % NZ) not in got
-                    assert wave_of(ny % NY, nz % NZ) == wave_of(dy, dz) + 1
-                    got.add((ny % NY, nz % NZ))
-        assert len(got) == SLOTS - 1 and (0, 0) not in got
-
-
-check_tree()
+ORDER = weight_order()
 
 
 def nt(a, b):
@@ -104,7 +122,7 @@
 
 def kernel(h_ref, g_ref, xown_ref, pu_ref, pd_ref, m_ref, v_ref,
            w_out, m_out, v_out,
-           xa, xb, h0, g1, h1, g0, xo, pq, mv, vv,
+           xw, h0, g1, h1, g0, xo, pq, mv, vv,
            act0, act1, gp0, dz0, dz1,
            part, rd, lbuf, rbuf, mid,
            rr, rmid, rl, rrt, zq, zbuf, res,
@@ -145,8 +163,7 @@
         local.append(copy)
 
     for layer in (0, 1):
-        stage(xown_ref.at[layer, :, pl.ds(0, KA)], xa.at[layer, 0])
-        stage(xown_ref.at[layer, :, pl.ds(KA, model - KA)], xb.at[layer, 0])
+        stage(xown_ref.at[layer], xw.at[layer, 0])
     stage(h_ref, h0.at[0, 0])
     stage(g_ref, g1.at[0, 0])
     stage(xown_ref, xo)
@@ -157,41 +174,37 @@
     stage(v_ref, vv)
 
     barrier = pltpu.get_barrier_semaphore()
-    partners = [partner, nbr["xp"], nbr["xm"], nbr["yp"], nbr["ym"]] + zdev[1:]
+    cross = {"xp": dev(z, y, x + 1, 1 - core), "xm": dev(z, y, x + NX - 1, 1 - core)}
+    partners = [partner] + list(nbr.values()) + list(cross.values())
     for target in partners:
         pl.semaphore_signal(barrier, inc=1, device_id=(target,), device_id_type=pl.DeviceIdType.MESH)
     pl.semaphore_wait(barrier, len(partners))
     for copy in local:
         copy.wait()
 
-    wparts = (xa, xb)
-
-    def w_issue(layer, prt, dy, dz):
-        buf = wparts[prt]
-        for direction, ny, nz in forwards(prt, dy, dz):
-            remote(buf.at[layer, slot(dy, dz)], buf.at[layer, slot(ny, nz)],
-                   w_send.at[layer, prt], w_recv.at[layer, prt, slot(ny, nz)], nbr[direction]).start()
-
-    def w_own(layer):
-        w_issue(layer, 0, 0, 0)
-        w_issue(layer, 1, 0, 0)
-
-    def w_wave(layer, wave):
-        for dy in range(NY):
-            for dz in range(NZ):
-                if wave_of(dy, dz) == wave:
-                    for prt in (0, 1):
-                        s = slot(dy, dz)
-                        buf = wparts[prt]
-                        remote(buf.at[layer, s], buf.at[layer, s], w_send.at[layer, prt],
-                               w_recv.at[layer, prt, s], partner).wait_recv()
-                        w_issue(layer, prt, dy, dz)
+    def piece(layer, s, prt):
+        first, columns, _, _ = PARTS[prt]
+        return xw.at[layer, s, :, pl.ds(first, columns)]
+
+    def w_step(event):
+        _, kind, layer, prt, dy, dz, direction, ny, nz = event
+        here = piece(layer, slot(dy, dz), prt)
+        if kind == "wait":
+            remote(here, here, w_send.at[layer, prt], w_recv.at[layer, prt, slot(dy, dz)], partner).wait_recv()
+        else:
+            remote(here, piece(layer, slot(ny, nz), prt), w_send.at[layer, prt],
+                   w_recv.at[layer, prt, slot(ny, nz)], nbr[direction]).start()
+
+    pending = list(ORDER)
+
+    def pump(until):
+        while pending and pending[0][0] <= until:
+            w_step(pending.pop(0))
 
     def w_drain(layer):
-        for prt in (0, 1):
-            buf = wparts[prt]
-            remote(buf.at[layer, pl.ds(1, SLOTS - 1)], buf.at[layer, pl.ds(1, SLOTS - 1)],
-                   w_send.at[layer, prt], w_recv.at[layer, prt, 0], partner).wait_send()
+        for prt, (first, columns, _, _) in enumerate(PARTS):
+            ref = xw.at[layer, pl.ds(1, SLOTS - 1), :, pl.ds(first, columns)]
+            remote(ref, ref, w_send.at[layer, prt], w_recv.at[layer, prt, 0], partner).wait_send()
 
     half = tok // 2
     drains = []
@@ -222,24 +235,23 @@
             lo, hi = pl.ds(0, half), pl.ds(half, half)
             self.arrived(0, b.at[0, 3])
             self.go(3, b.at[0, 3, lo], b.at[0, 2, lo], nbr["xp"])
+            self.go(7, b.at[0, 3, lo], b.at[1, 2, lo], cross["xp"])
             self.go(5, b.at[0, 3], b.at[1, 3], partner)
             self.arrived(1, b.at[0, 1])
             self.go(4, b.at[0, 1, hi], b.at[0, 2, hi], nbr["xm"])
+            self.go(8, b.at[0, 1, hi], b.at[1, 2, hi], cross["xm"])
             self.go(6, b.at[0, 1], b.at[1, 1], partner)
 
-        def last(self):
+        def finish(self):
             b = self.buf
             lo, hi = pl.ds(0, half), pl.ds(half, half)
-            self.arrived(3, b.at[0, 2, lo])
-            self.arrived(4, b.at[0, 2, hi])
-            self.go(7, b.at[0, 2], b.at[1, 2], partner)
-
-        def finish(self):
-            b = self.buf
             self.arrived(2, b.at[1, 0])
             self.arrived(5, b.at[1, 3])
             self.arrived(6, b.at[1, 1])
-            self.arrived(7, b.at[1, 2])
+            self.arrived(3, b.at[0, 2, lo])
+            self.arrived(4, b.at[0, 2, hi])
+            self.arrived(7, b.at[1, 2, lo])
+            self.arrived(8, b.at[1, 2, hi])
 
     class Reduce:
         def __init__(self, index):
@@ -258,38 +270,42 @@
 
         def to_partner(self):
             i = self.index
-            self.go(0, part.at[i, 1], rd.at[i], partner)
+            for dx in (2, 1, 3, 0):
+                self.go(dx, part.at[i, 1, dx], rd.at[i, dx], partner)
 
         def ring(self):
             i = self.index
             lo, hi = pl.ds(0, half), pl.ds(half, half)
-            self.arrived(0, rd.at[i])
-            part[i, 0, 2] = part[i, 0, 2] + rd[i, 2]
-            self.go(1, part.at[i, 0, 2, lo], mid.at[i, lo], nbr["xp"])
-            self.go(2, part.at[i, 0, 2, hi], mid.at[i, hi], nbr["xm"])
-            part[i, 0, 1] = part[i, 0, 1] + rd[i, 1]
-            self.go(3, part.at[i, 0, 1, hi], lbuf.at[i, hi], nbr["xp"])
-            part[i, 0, 3] = part[i, 0, 3] + rd[i, 3]
-            self.go(4, part.at[i, 0, 3, lo], rbuf.at[i, lo], nbr["xm"])
-            part[i, 0, 0] = part[i, 0, 0] + rd[i, 0]
+            def add(dx):
+                self.arrived(dx, rd.at[i, dx])
+                part[i, 0, dx] = part[i, 0, dx] + rd[i, dx]
+
+            add(2)
+            self.go(4, part.at[i, 0, 2, lo], mid.at[i, lo], nbr["xp"])
+            self.go(5, part.at[i, 0, 2, hi], mid.at[i, hi], nbr["xm"])
+            add(1)
+            self.go(6, part.at[i, 0, 1, hi], lbuf.at[i, hi], nbr["xp"])
+            add(3)
+            self.go(7, part.at[i, 0, 3, lo], rbuf.at[i, lo], nbr["xm"])
+            add(0)
 
         def ring_second(self):
             i = self.index
             lo, hi = pl.ds(0, half), pl.ds(half, half)
-            self.arrived(1, mid.at[i, lo])
+            self.arrived(4, mid.at[i, lo])
             part[i, 0, 1, lo] = part[i, 0, 1, lo] + mid[i, lo]
-            self.go(5, part.at[i, 0, 1, lo], lbuf.at[i, lo], nbr["xp"])
-            self.arrived(2, mid.at[i, hi])
+            self.go(8, part.at[i, 0, 1, lo], lbuf.at[i, lo], nbr["xp"])
+            self.arrived(5, mid.at[i, hi])
             part[i, 0, 3, hi] = part[i, 0, 3, hi] + mid[i, hi]
-            self.go(6, part.at[i, 0, 3, hi], rbuf.at[i, hi], nbr["xm"])
+            self.go(9, part.at[i, 0, 3, hi], rbuf.at[i, hi], nbr["xm"])
 
         def total(self):
             i = self.index
             lo, hi = pl.ds(0, half), pl.ds(half, half)
-            self.arrived(3, lbuf.at[i, hi])
-            self.arrived(4, rbuf.at[i, lo])
-            self.arrived(5, lbuf.at[i, lo])
-            self.arrived(6, rbuf.at[i, hi])
+            self.arrived(6, lbuf.at[i, hi])
+            self.arrived(7, rbuf.at[i, lo])
+            self.arrived(8, lbuf.at[i, lo])
+            self.arrived(9, rbuf.at[i, hi])
             return part[i, 0, 0] + lbuf[i] + rbuf[i]
 
     class Scatter:
@@ -351,12 +367,7 @@
     per = CH // ROWS
 
     def xrows(layer, i):
-        a = xa[layer, pl.ds(i * per, per)].reshape(CH, KA)
-        b = xb[layer, pl.ds(i * per, per)].reshape(CH, model - KA)
-        return a, b
-
-    def against(x2, acts):
-        return nt(x2[0], acts[:, :KA]) + nt(x2[1], acts[:, KA:])
+        return xw[layer, pl.ds(i * per, per)].reshape(CH, model)
 
     def row_in_slot():
         r = lax.broadcasted_iota(jnp.int32, (CH, group), 0)
@@ -391,16 +402,10 @@
         return pl.ds(pl.multiple_of(i * CH, CH), CH)
 
     def products(act_ref, layer, out_index):
-        def body(j):
-            for q in range(1, -1, -1):
-                pass
         for cc in (1, 0):
             toks = pl.ds(cc * (group // 2), group // 2)
             lhs = act_ref[:, toks]
-            a = xa[layer].reshape(rows, KA)
-            b = xb[layer].reshape(rows, model - KA)
-            part[out_index, cc, :, :, pl.ds(0, KA)] = tn(lhs, a).reshape(NX, tok, KA)
-            part[out_index, cc, :, :, pl.ds(KA, model - KA)] = tn(lhs, b).reshape(NX, tok, model - KA)
+            part[out_index, cc] = tn(lhs, xw[layer].reshape(rows, model)).reshape(NX, tok, model)
             if cc == 1:
                 Reduce(out_index).to_partner()
 
@@ -412,56 +417,49 @@
         gq = nn(flat(g_ref2), pq[layer])[:, rank:]
         return jnp.concatenate(split(hp), axis=1), jnp.concatenate(split(gq), axis=1)
 
+    done = [max(e[0] for e in ORDER if e[2] == layer) for layer in (0, 1)]
     gather_h, gather_g = Gather(h0, 0), Gather(g1, 1)
-    w_own(0)
+    pump(0.0)
     gather_h.start()
-    w_own(1)
     gather_g.start()
-    w_wave(0, 1)
+    pump(4.0)
     gather_h.middle()
-    w_wave(0, 2)
-    w_wave(1, 1)
-    gather_h.last()
+    pump(6.0)
     gather_g.middle()
-    w_wave(0, 3)
-    w_wave(1, 2)
-    gather_g.last()
+    pump(9.0)
     gather_h.finish()
-    w_wave(0, 4)
-    w_wave(1, 3)
     gather_g.finish()
-    w_wave(0, 5)
-    w_wave(1, 4)
-    w_wave(0, 6)
-
-    acts = flat(h0)
+    pump(done[0])
 
     @chunks
     def _(i):
-        zt = against(xrows(0, i), flat(h0))
+        zt = nt(xrows(0, i), flat(h0))
         value, slope = gelu_pair(zt)
         gp0[block(i), :] = slope
         act0[block(i), :] = to_down(value).astype(BF16)
 
+    pump(done[0] + 1.3)
     products(act0, 0, 0)
-    w_wave(1, 5)
+    pump(done[0] + 2.5)
     reduce0 = Reduce(0)
     reduce0.ring()
+    pump(done[0] + 5.0)
     reduce0.ring_second()
-    w_wave(1, 6)
+    pump(done[0] + 8.0)
     h1[0, 0] = (h0[0, 0].astype(F32) + reduce0.total()).astype(BF16)
     gather1 = Gather(h1, 2)
     gather1.start()
+    pump(done[0] + 11.0)
     gather1.middle()
-    gather1.last()
+    pump(done[1])
     gather1.finish()
 
     @chunks
     def _(i):
         x2 = xrows(1, i)
-        value, slope = gelu_pair(against(x2, flat(h1)))
+        value, slope = gelu_pair(nt(x2, flat(h1)))
         act1[block(i), :] = to_down(value).astype(BF16)
-        dpost = to_up(against(x2, flat(g1)))
+        dpost = to_up(nt(x2, flat(g1)))
         dz1[block(i), :] = mask_up(slope * dpost).astype(BF16)
 
     products(dz1, 1, 1)
@@ -479,22 +477,21 @@
 
     reduce1.ring()
     reduce1.ring_second()
+    g0[0, 0] = (g1[0, 0].astype(F32) + reduce1.total()).astype(BF16)
+    gather0 = Gather(g0, 3)
+    gather0.start()
     projected(1, dz1, act1, h1, g1)
     scatter1 = Scatter(1)
     scatter1.ring()
-    g0[0, 0] = (g1[0, 0].astype(F32) + reduce1.total()).astype(BF16)
-    gather0 = Gather(g0, 3)
-    gather0.start()
-    scatter1.ring_second()
     gather0.middle()
-    gather0.last()
     gather0.finish()
 
     @chunks
     def _(i):
-        dpost = to_up(against(xrows(0, i), flat(g0)))
+        dpost = to_up(nt(xrows(0, i), flat(g0)))
         dz0[block(i), :] = mask_up(gp0[block(i), :] * dpost).astype(BF16)
 
+    scatter1.ring_second()
     projected(0, dz0, act0, h0, g0)
     scatter0 = Scatter(0)
     scatter0.ring()
@@ -535,7 +532,6 @@
 def fused_step(act_in, grad_top, xown, proj_up, proj_down, mom, var):
     tok, model = act_in.shape
     layers, _, rank = proj_up.shape
-    kb = model - KA
     group = NC * NX * tok
     rows = SLOTS * ROWS
     dma = pltpu.SemaphoreType.DMA
@@ -543,7 +539,7 @@
     vm = pltpu.VMEM
     blk = (NC, NX, tok, model)
     scratch = [
-        vm((2, SLOTS, ROWS, KA), BF16), vm((2, SLOTS, ROWS, kb), BF16),
+        vm((2, SLOTS, ROWS, model), BF16),
         vm(blk, BF16), vm(blk, BF16), vm(blk, BF16), vm(blk, BF16),
         vm((2, ROWS, model), BF16), vm((2, model, 2 * rank), BF16), vm((2, ROWS, rank), F32), vm((2, ROWS, rank), F32),
         vm((rows, group), BF16), vm((rows, group), BF16), vm((rows, group), F32), vm((rows, group), BF16), vm((rows, group), BF16),
@@ -551,7 +547,7 @@
         vm((2, NY, NZ, ROWS, rank), F32), vm((2, NZ, ROWS, rank), F32), vm((2, NZ, ROWS, rank), F32), vm((2, NZ, ROWS, rank), F32),
         vm((2, NZ, ROWS, rank), F32), vm((2, NZ, ROWS, rank), F32), vm((2, ROWS, rank), F32),
         vm((2, ROWS, model), BF16), vm((2, ROWS, rank), F32), vm((2, ROWS, rank), F32),
-        dma((13,)), dma((2, 2)), dma((2, 2, SLOTS)), dma((4, 8)), dma((4, 8)), dma((2, 7)), dma((2, 7)),
+        dma((11,)), dma((2, len(PARTS))), dma((2, len(PARTS), SLOTS)), dma((4, 9)), dma((4, 9)), dma((2, 10)), dma((2, 10)),
         dma((2, 6)), dma((2, 6)), dma((2, NZ)), dma((2, NZ)), dma((3,)),
     ]
     return pl.pallas_call(

time: 105 us -> 105 us (level)
  no operation moved by 1% of the time
where the time goes in v2:
time: 105 us; the launch traced here: 104 us
  Pallas kernels  95.3 us (91%)
  local copies, waits for them, and re-layouts  8.21 us (8%)
    pallas_call x1, Pallas kernels, fused_step(): pl.pallas_call(kernel, name='galore_step', out_shape=(jax.ShapeDtypeStruc...  95.3 us
    unnamed x20, local copies, waits for them, and re-layouts  7.19 us

profile of v2, /device:TPU:2, one launch (start us, length us, event | category | flops | bytes accessed | tf_op | source)
XLA Modules:
  0.0 104.4 jit_solution(15287925574182313853)
XLA Ops:
  0.6 0.1 pad.8.clone
  0.7 0.0 copy-start.4
  0.7 0.1 pad.5.clone
  0.8 0.0 copy-start.2
  0.8 0.7 copy.19
  1.5 0.0 copy-done.4
  1.5 0.0 copy-start
  1.6 0.8 copy_bitcast_fusion.1
  2.4 0.1 maximum_maximum_fusion.2
  2.5 0.9 copy.31
  3.4 0.9 copy.17
  4.3 0.1 maximum_maximum_fusion.xown_ref
  4.4 0.0 copy-done.2
  4.4 0.0 copy-done.1
  4.4 0.0 copy-done
  4.4 0.0 copy-start.3
  4.4 0.8 copy-done.3
  5.2 95.3 %galore_step.1 = (bf16[2,40,896]{2,1,0:T(8,128)(2,1)S(1)}, f32[2,40,128]{2,1,0:T(8,128)S(1)}, f32[2,40,128]{2,1,0:T(8,128)S(1)}) custom-call(bf16[32,896]{1,0:T(8,128)(2,1)S(1)} %copy-done.2, bf16[32,896]{1,0:T(8,128)(2,1)S(1)} %copy-done.3, bf16[2,40,896]{2,1,0:T(8,128)(2,1)S(1)} %maximum_maximum_fusion.xown_ref, bf16[2,896,128]{2,1,0:T(8,128)(2,1)S(1)} %copy-done, ...), custom_call_target="tpu_custom_call" | custom-call | tf_op jit(solution)/shard_map/galore_step/pallas_call | solution.py:553
  100.6 0.7 copy.23
  101.3 0.6 copy.26
  101.9 0.6 copy.24
  102.5 0.6 copy.27
  103.1 0.6 copy.25
  103.7 0.7 copy.22
  (7 shorter events, 0.0 us)
Async XLA Ops:
  0.7 0.8 copy-start.4
  0.8 3.6 %copy-start.2 = (bf16[32,896]{1,0:T(8,128)(2,1)S(1)}, bf16[32,896]{1,0:T(8,128)(2,1)}, u32[]{:S(2)}) copy-start(bf16[32,896]{1,0:T(8,128)(2,1)} %h_ref.1) | copy-start | bytes 172036
  1.5 2.8 %copy-start.1 = (bf16[2,896,128]{2,1,0:T(8,128)(2,1)S(1)}, bf16[2,896,128]{2,1,0:T(8,128)(2,1)}, u32[]{:S(2)}) copy-start(bf16[2,896,128]{2,1,0:T(8,128)(2,1)} %pd_ref.1) | copy-start | bytes 1376260
  1.5 2.8 %copy-start = (bf16[2,896,128]{2,1,0:T(8,128)(2,1)S(1)}, bf16[2,896,128]{2,1,0:T(8,128)(2,1)}, u32[]{:S(2)}) copy-start(bf16[2,896,128]{2,1,0:T(8,128)(2,1)} %pu_ref.1) | copy-start | bytes 1376260
  4.4 0.8 copy-start.3
